TPU v7x, 32 devices: a whole 2x2x4 slice. The times are simulated.
32 devices in a mesh: len: 2 (over x), wid: 4 (over z), dep: 4 (over y, core).
Axes of the slice: x: 2, y: 2, z: 4, core: 2. Of those that a mesh axis runs over, the one named last changes fastest.
Arguments:
- coords: float32 [3, 32768], P(None, ('len', 'wid', 'dep')), may hold values from -3 to 3
- velocity: float32 [3, 32768], P(None, ('len', 'wid', 'dep')), may hold values from -6 to 6
- node_mass: float32 [32768], P(('len', 'wid', 'dep')), may hold values from 0.5 to 2
- corner_nodes: int32 [4, 32768], P(None, ('len', 'wid', 'dep')), may hold values from 0 to 1151, as said below
- shape_grad: float32 [8, 32768], P(None, ('len', 'wid', 'dep')), may hold values from -5 to 5
- frame_angles: float32 [2, 32768], P(None, ('len', 'wid', 'dep')), may hold values from -3.140625 to 3.140625
- volume: float32 [32768], P(('len', 'wid', 'dep')), may hold values from 0.5 to 2
- stress: float32 [3, 32768], P(None, ('len', 'wid', 'dep')), may hold values from -5 to 5
- send_nodes: int32 [32, 16, 256], P(('len', 'wid', 'dep')), may hold values from 0 to 1023
- tile_count: int32 [32], P(('len', 'wid', 'dep')), may hold values from 1 to 4, as said below
- tile_nodes: int32 [128, 128], P(('len', 'wid', 'dep')), may hold values from 0 to 4095
- tile_facets: int32 [4, 128, 128], P(None, ('len', 'wid', 'dep')), may hold values from 0 to 4095
- pair_mask: int32 [128, 128, 128], P(('len', 'wid', 'dep')), may hold values 0 or 1
Outputs:
- coords_out: float32 [3, 32768], P(None, ('len', 'wid', 'dep'))
- velocity_out: float32 [3, 32768], P(None, ('len', 'wid', 'dep'))
- stress_out: float32 [3, 32768], P(None, ('len', 'wid', 'dep'))
Inputs may be any that keep to these rules, and one draw needn't show every extreme that they name: `corner_nodes`: for the element at device-local position i (i = e mod 1024), every entry lies from (i // 128) * 128 to (i // 128) * 128 + 2 * 128 - 1. An entry j below 1024 names the element device's own node j; an entry 1024 + i names node i of the next device in the order len, wid, dep, the last device's next being the first. `send_nodes`: entry [p, g, k] is a node of device p, by its local number, sent to device g of p's slab; nodes may repeat. `tile_count`: some device has 4 live tiles in every draw; a device's tiles at and past its count are not used. `tile_nodes`: slot g * 256 + k of the tile's device is slot k of what device g of its slab sends it. `tile_facets`: slots as for tile_nodes, one for each of a facet's four corners.
All inputs are finite; a program needn't handle non-finite values. No bound on the sum of `pair_mask` on one device may be relied on, other than what follows from the above.
Results may differ from a plain program's by a relative error of at most 0.0003.
Values sent between devices are 32-bit elements; how exact they have to be, the bound alone decides.
A program may use at most 64 MiB of HBM per device.

v0:
```python
import math
import jax
import jax.numpy as jnp
from jax import lax
from jax.sharding import PartitionSpec as P

RIM = 128
STEPS = 2
TIME_STEP = 0.1
YOUNG_MOD = 1.0
POISSON = 0.3
HOURGLASS = 0.1
RADIUS_SQ = 1.0
STIFFNESS = 0.1
DAMPING = 0.05


def from_behind(value, axis, steps):
    count = lax.axis_size(axis)
    pairs = [(source, (source + steps) % count) for source in range(count)]
    return lax.ppermute(value, axis, pairs)


def frame_vectors(frame_angles):
    polar_angle = frame_angles[0]
    azimuth = frame_angles[1]
    axis_one = jnp.stack(
        [
            jnp.cos(polar_angle) * jnp.cos(azimuth),
            jnp.cos(polar_angle) * jnp.sin(azimuth),
            -jnp.sin(polar_angle),
        ]
    )
    axis_two = jnp.stack([-jnp.sin(azimuth), jnp.cos(azimuth), jnp.zeros_like(azimuth)])
    return (axis_one, axis_two)


def element_forces(corner_vel, shape_grad, axis_one, axis_two, volume, stress):
    grad_x = shape_grad[:4]
    grad_y = shape_grad[4:]
    along_one = jnp.sum(axis_one[:, None, :] * corner_vel, axis=0)
    along_two = jnp.sum(axis_two[:, None, :] * corner_vel, axis=0)
    rate_xx = jnp.sum(grad_x * along_one, axis=0)
    rate_yy = jnp.sum(grad_y * along_two, axis=0)
    rate_xy = jnp.sum(grad_y * along_one + grad_x * along_two, axis=0)
    factor = TIME_STEP * YOUNG_MOD / (1.0 - POISSON * POISSON)
    sigma_xx = stress[0] + factor * (rate_xx + POISSON * rate_yy)
    sigma_yy = stress[1] + factor * (POISSON * rate_xx + rate_yy)
    sigma_xy = stress[2] + factor * 0.5 * (1.0 - POISSON) * rate_xy
    hourglass_mode = jnp.array([1.0, -1.0, 1.0, -1.0], jnp.float32)[:, None]
    hourglass_rate = jnp.sum(hourglass_mode[None] * corner_vel, axis=1)
    force_one = -volume * (grad_x * sigma_xx + grad_y * sigma_xy)
    force_two = -volume * (grad_y * sigma_yy + grad_x * sigma_xy)
    corner_force = (
        axis_one[:, None] * force_one[None]
        + axis_two[:, None] * force_two[None]
        - HOURGLASS * volume * hourglass_mode[None] * hourglass_rate[:, None]
    )
    return (corner_force, jnp.stack([sigma_xx, sigma_yy, sigma_xy]))


def tile_forces(node_coordinates, node_velocities, corner_pos, corner_vel, pair_bits, live_row):
    facet_centroid = 0.25 * jnp.sum(corner_pos, axis=1)
    centroid_velocity = 0.25 * jnp.sum(corner_vel, axis=1)
    inner_product = jnp.einsum(
        "ywq,ywk->wqk", node_coordinates, facet_centroid, precision=lax.Precision.HIGHEST
    )
    distance = (
        jnp.sum(node_coordinates * node_coordinates, axis=0)[:, :, None]
        + jnp.sum(facet_centroid * facet_centroid, axis=0)[:, None, :]
        - 2.0 * inner_product
    )
    corner_weight = (
        pair_bits.astype(jnp.float32)
        * live_row[:, None, None]
        * jnp.maximum(RADIUS_SQ - distance, 0.0)
    )
    row_sum = jnp.sum(corner_weight, axis=2)
    col_sum = jnp.sum(corner_weight, axis=1)
    gathered_positions = jnp.einsum(
        "yml,mjl->ymj", facet_centroid, corner_weight, precision=lax.Precision.HIGHEST
    )
    gathered_velocities = jnp.einsum(
        "yml,mjl->ymj", centroid_velocity, corner_weight, precision=lax.Precision.HIGHEST
    )
    node_force = STIFFNESS * (row_sum * node_coordinates - gathered_positions) - DAMPING * (
        row_sum * node_velocities - gathered_velocities
    )
    outgoing_positions = jnp.einsum(
        "ewo,woj->ewj", node_coordinates, corner_weight, precision=lax.Precision.HIGHEST
    )
    outgoing_velocities = jnp.einsum(
        "ewo,woj->ewj", node_velocities, corner_weight, precision=lax.Precision.HIGHEST
    )
    facet_force = STIFFNESS * (outgoing_positions - col_sum * facet_centroid) - DAMPING * (
        outgoing_velocities - col_sum * centroid_velocity
    )
    return (node_force, -0.25 * facet_force)


def split_parts(values):
    first = lax.optimization_barrier(values.astype(jnp.bfloat16))
    rest = values - first.astype(jnp.float32)
    second = lax.optimization_barrier(rest.astype(jnp.bfloat16))
    third = (rest - second.astype(jnp.float32)).astype(jnp.bfloat16)
    return jnp.concatenate([first, second, third], axis=0)


def put_rows(values, index, total):
    chans, count = values.shape
    low_span = math.gcd(total, 128)
    high_span = total // low_span
    block = math.gcd(count, 1024)
    turns = count // block
    parts = jnp.transpose(split_parts(values).reshape(3 * chans, turns, block), (1, 0, 2))
    index_blocks = index.reshape(turns, block)
    low_iota = jnp.arange(low_span, dtype=jnp.int32)
    high_iota = jnp.arange(high_span, dtype=jnp.int32)

    def add_block(running, pieces):
        part, ids = pieces
        low_match = ids[:, None] % low_span == low_iota[None, :]
        spread_rows = jnp.where(low_match[None], part[:, :, None], jnp.zeros((), jnp.bfloat16))
        high_match = (ids[:, None] // low_span == high_iota[None, :]).astype(jnp.bfloat16)
        return (
            running
            + jnp.einsum(
                "mh,kml->khl", high_match, spread_rows, preferred_element_type=jnp.float32
            ),
            None,
        )

    summed, unused = lax.scan(
        add_block, jnp.zeros((3 * chans, high_span, low_span), jnp.float32), (parts, index_blocks)
    )
    return summed.reshape(3, chans, total).sum(axis=0)


def window_layout(corner_nodes, span):
    elements = corner_nodes.shape[1]
    blocks = elements // span
    group = math.gcd(blocks, 8)
    rounds = blocks // group
    starts = (jnp.arange(blocks, dtype=jnp.int32) * span)[None, :, None]
    local_ids = (corner_nodes.reshape(4, blocks, span) - starts).reshape(4, rounds, group, span)
    return (jnp.transpose(local_ids, (1, 0, 2, 3)), blocks, group, rounds)


def window_gather(extended, corner_nodes, span):
    local_ids, blocks, group, rounds = window_layout(corner_nodes, span)
    pieces = extended.reshape(3, blocks + 1, span)
    windows = jnp.concatenate([pieces[:, :-1], pieces[:, 1:]], axis=2)
    parts = jnp.transpose(split_parts(windows).reshape(9, rounds, group, 2 * span), (1, 0, 2, 3))
    window_iota = jnp.arange(2 * span, dtype=jnp.int32)

    def pick_round(items):
        part, ids = items
        onehot = (ids[..., None] == window_iota).astype(jnp.bfloat16)
        return jnp.einsum("abij,kbj->kabi", onehot, part, preferred_element_type=jnp.float32)

    picked = lax.map(pick_round, (parts, local_ids))
    picked = jnp.transpose(picked, (1, 2, 0, 3, 4)).reshape(3, 3, 4, blocks * span)
    return picked.sum(axis=0)


def window_put(corner_force, corner_nodes, span):
    local_ids, blocks, group, rounds = window_layout(corner_nodes, span)
    parts = jnp.transpose(
        split_parts(corner_force).reshape(9, 4, rounds, group, span), (2, 0, 1, 3, 4)
    )
    window_iota = jnp.arange(2 * span, dtype=jnp.int32)

    def put_round(items):
        part, ids = items
        onehot = (ids[..., None] == window_iota).astype(jnp.bfloat16)
        return jnp.einsum("abij,kabi->kbj", onehot, part, preferred_element_type=jnp.float32)

    sums = lax.map(put_round, (parts, local_ids))
    sums = jnp.transpose(sums, (1, 0, 2, 3)).reshape(3, 3, blocks, 2 * span).sum(axis=0)
    near_half = jnp.pad(sums[:, :, :span], ((0, 0), (0, 1), (0, 0)))
    far_half = jnp.pad(sums[:, :, span:], ((0, 0), (1, 0), (0, 0)))
    return (near_half + far_half).reshape(3, (blocks + 1) * span)


def spread_tiles(node_force, facet_share, tile_nodes, tile_facets, total):
    corner_share = jnp.broadcast_to(facet_share[:, None], (3, 4) + facet_share.shape[1:])
    values = jnp.concatenate([node_force.reshape(3, -1), corner_share.reshape(3, -1)], axis=1)
    index = jnp.concatenate([tile_nodes.reshape(-1), tile_facets.reshape(-1)], axis=0)
    return put_rows(values, index, total)


def ship_out(positions, velocities):
    recv_pos, recv_vel = (
        lax.all_to_all(positions, ("wid", "dep"), split_axis=1, concat_axis=1, tiled=True),
        lax.all_to_all(velocities, ("wid", "dep"), split_axis=1, concat_axis=1, tiled=True),
    )
    return (recv_pos.reshape(3, -1), recv_vel.reshape(3, -1))


def ship_back(buffer, capacity):
    group_size = lax.axis_size("wid") * lax.axis_size("dep")
    returned = lax.all_to_all(
        buffer.reshape(3, group_size, capacity),
        ("wid", "dep"),
        split_axis=1,
        concat_axis=1,
        tiled=True,
    )
    return returned


def contact_buffer(recv_pos, recv_vel, tile_nodes, tile_facets, pair_mask, live_tiles):
    total = recv_pos.shape[1]
    node_force, facet_share = tile_forces(
        recv_pos[:, tile_nodes],
        recv_vel[:, tile_nodes],
        recv_pos[:, tile_facets],
        recv_vel[:, tile_facets],
        pair_mask,
        live_tiles,
    )
    return spread_tiles(node_force, facet_share, tile_nodes, tile_facets, total)


def per_device(
    coords,
    velocity,
    node_mass,
    corner_nodes,
    shape_grad,
    frame_angles,
    volume,
    stress,
    send_nodes,
    tile_count,
    tile_nodes,
    tile_facets,
    pair_mask,
):
    axis_one, axis_two = frame_vectors(frame_angles)
    slot_rows = send_nodes[0]
    capacity = slot_rows.shape[1]
    slot_flat = slot_rows.reshape(-1)
    tile_slots = pair_mask.shape[0]
    live_tiles = (jnp.arange(tile_slots, dtype=jnp.int32) < tile_count[0]).astype(jnp.float32)
    local_count = coords.shape[1]
    for repeat in range(STEPS):
        ghosts = from_behind(velocity[:, :RIM], ("len", "wid", "dep"), -1)
        extended = jnp.concatenate([velocity, ghosts], axis=1)
        corner_vel = window_gather(extended, corner_nodes, RIM)
        corner_force, stress = element_forces(
            corner_vel, shape_grad, axis_one, axis_two, volume, stress
        )
        nodal_sum = window_put(corner_force, corner_nodes, RIM)
        returned = from_behind(nodal_sum[:, local_count:], ("len", "wid", "dep"), 1)
        internal = nodal_sum[:, :local_count] + jnp.pad(returned, ((0, 0), (0, local_count - RIM)))
        recv_pos, recv_vel = ship_out(coords[:, slot_rows], velocity[:, slot_rows])
        buffer = contact_buffer(recv_pos, recv_vel, tile_nodes, tile_facets, pair_mask, live_tiles)
        answer = ship_back(buffer, capacity)
        contact = put_rows(answer.reshape(3, -1), slot_flat, local_count)
        velocity = velocity + TIME_STEP * (internal + contact) / node_mass
        coords = coords + TIME_STEP * velocity
    return (coords, velocity, stress)


def solution(mesh):
    placed = (
        P(None, ("len", "wid", "dep")),
        P(None, ("len", "wid", "dep")),
        P(("len", "wid", "dep")),
        P(None, ("len", "wid", "dep")),
        P(None, ("len", "wid", "dep")),
        P(None, ("len", "wid", "dep")),
        P(("len", "wid", "dep")),
        P(None, ("len", "wid", "dep")),
        P(("len", "wid", "dep"), None, None),
        P(("len", "wid", "dep")),
        P(("len", "wid", "dep"), None),
        P(None, ("len", "wid", "dep"), None),
        P(("len", "wid", "dep"), None, None),
    )
    return jax.shard_map(
        per_device,
        mesh=mesh,
        in_specs=placed,
        out_specs=(
            P(None, ("len", "wid", "dep")),
            P(None, ("len", "wid", "dep")),
            P(None, ("len", "wid", "dep")),
        ),
        check_vma=False,
    )
```

profile of v0, /device:TPU:0, one launch (start us, length us, event | category | flops | bytes accessed | tf_op | source)
XLA Modules:
  0.0 197.0 jit_solution(1197763720123110898)
XLA Ops:
  2.4 10.8 %gather_fusion = f32[4096,3]{1,0:T(8,128)S(1)} fusion(f32[3,1024]{0,1:T(8,128)S(1)} %copy.159, s32[4096]{0:T(1024)S(1)} %broadcast_clamp_fusion), kind=kCustom, calls=%fused_computation | custom fusion | bytes 114688 | tf_op jit(solution)/shard_map/gather | solution.py:257
  13.2 1.2 copy.160
  14.5 7.4 %all-to-all-start = ((f32[3,16,256]{2,0,1:T(4,128)}), f32[3,16,256]{2,0,1:T(4,128)S(1)}, u32[]{:S(2)}, u32[]{:S(2)}) async-start(f32[3,16,256]{2,0,1:T(4,128)} %bitcast.19), calls=%async_computation | async-start | bytes 131072 | tf_op jit(solution)/shard_map/all_to_all | solution.py:194
  21.9 5.3 %collective-permute-start = (f32[3,128]{1,0:T(4,128)S(1)}, f32[3,128]{1,0:T(4,128)S(1)}, u32[]{:S(2)}, u32[]{:S(2)}) collective-permute-start(f32[3,128]{1,0:T(4,128)S(1)} %slice.69), channel_id=1, source_target_pairs={{0,31},{1,0},{2,1},{3,2},{4,3},{5,4},{6,5},{7,6},{8,7},{9,8},{10,9... | collective-permute-start | bytes 4616 | tf_op jit(solution)/shard_map/ppermute | solution.py:21
  30.5 10.8 %gather_fusion.3 = f32[4096,3]{1,0:T(8,128)S(1)} fusion(f32[3,1024]{0,1:T(8,128)S(1)} %copy.166, s32[4096]{0:T(1024)S(1)} %broadcast_clamp_fusion), kind=kCustom, calls=%fused_computation.3 | custom fusion | bytes 114688 | tf_op jit(solution)/shard_map/gather | solution.py:257
  41.3 1.2 copy.167
  42.7 1.4 fusion.100
  45.3 1.4 fusion.102
  47.4 3.5 %all-to-all-start.1 = ((f32[3,16,256]{2,0,1:T(4,128)}), f32[3,16,256]{2,0,1:T(4,128)S(1)}, u32[]{:S(2)}, u32[]{:S(2)}) async-start(f32[3,16,256]{2,0,1:T(4,128)} %bitcast.29), calls=%async_computation.1 | async-start | bytes 131072 | tf_op jit(solution)/shard_map/all_to_all | solution.py:195
  51.6 5.5 %gather_fusion.2 = f32[2048,3]{1,0:T(8,128)S(1)} fusion(f32[3,4096]{0,1:T(8,128)S(1)} %bitcast.286, s32[2048]{0:T(1024)S(1)} %broadcast_clamp_fusion.1), kind=kCustom, calls=%fused_computation.2 | custom fusion | bytes 57344 | tf_op jit(solution)/shard_map/gather | solution.py:217
  57.1 1.8 gather_fusion.1
  61.1 1.6 gather_fusion.4
  62.7 5.5 %gather_fusion.5 = f32[2048,3]{1,0:T(8,128)S(1)} fusion(f32[3,4096]{0,1:T(8,128)S(1)} %bitcast.291, s32[2048]{0:T(1024)S(1)} %broadcast_clamp_fusion.1), kind=kCustom, calls=%fused_computation.5 | custom fusion | bytes 57344 | tf_op jit(solution)/shard_map/gather | solution.py:218
  68.2 1.1 copy.163
  69.3 1.8 fusion.202
  71.0 1.1 copy.170
  74.5 8.7 %while.68 = (s32[]{:T(128)}, f32[9,32,128]{2,1,0:T(8,128)S(1)}, s32[5,512]{1,0:T(8,128)}, bf16[5,9,512]{2,1,0:T(8,128)(2,1)S(1)}, s32[]{:T(128)}, /*index=5*/s32[]{:T(128)}) while((s32[]{:T(128)}, f32[9,32,128]{2,1,0:T(8,128)S(1)}, s32[5,512]{1,0:T(8,128)}, bf16[5,9,512]{2,1,0:T(8,128)(2,1)S(1)}, s32[]{:T(128)}, ...), condition=%wide.region_15.16_spmd.clone, body=%wide.region_14.15_spmd.clone.sunk | while | flops 38503936 | bytes 468063 | solution.py:133
  84.0 6.0 %all-to-all-start.2 = ((f32[3,16,256]{2,0,1:T(4,128)}), f32[3,16,256]{2,0,1:T(4,128)S(1)}, u32[]{:S(2)}, u32[]{:S(2)}) async-start(f32[3,16,256]{2,0,1:T(4,128)} %bitcast.39), calls=%async_computation.2 | async-start | bytes 131072 | tf_op jit(solution)/shard_map/all_to_all | solution.py:202
  90.5 6.4 %all-to-all-done.2 = f32[3,16,256]{2,0,1:T(4,128)S(1)} async-done(((f32[3,16,256]{2,0,1:T(4,128)}), f32[3,16,256]{2,0,1:T(4,128)S(1)}, u32[]{:S(2)}, u32[]{:S(2)}) %all-to-all-start.2) | async-done | bytes 49184 | tf_op jit(solution)/shard_map/all_to_all | solution.py:202
  97.1 6.7 %while.69 = (s32[]{:T(128)}, f32[9,8,128]{2,1,0:T(8,128)S(1)}, s32[4,1024]{1,0:T(4,128)S(1)}, bf16[4,9,1024]{2,1,0:T(8,128)(2,1)S(1)}, s32[]{:T(128)}, /*index=5*/s32[]{:T(128)}) while((s32[]{:T(128)}, f32[9,8,128]{2,1,0:T(8,128)S(1)}, s32[4,1024]{1,0:T(4,128)S(1)}, bf16[4,9,1024]{2,1,0:T(8,128)(2,1)S(1)}, s32[]{:T(128)}, ...), condition=%wide.region_18.19_spmd.clone, body=%wide.region_17.18_spmd.clone.sunk | while | flops 20231172 | bytes 419935 | solution.py:133
  97.4 1.4 fusion.235
  99.1 1.4 fusion.235
  100.7 1.4 fusion.235
  102.4 1.4 fusion.235
  104.8 10.8 %gather_fusion.6 = f32[4096,3]{1,0:T(8,128)S(1)} fusion(f32[3,1024]{0,1:T(8,128)S(1)} %copy.182, s32[4096]{0:T(1024)S(1)} %broadcast_clamp_fusion), kind=kCustom, calls=%fused_computation.6 | custom fusion | bytes 114688 | tf_op jit(solution)/shard_map/gather | solution.py:257
  115.6 1.2 copy.183
  116.8 3.7 %all-to-all-start.3 = ((f32[3,16,256]{2,0,1:T(4,128)}), f32[3,16,256]{2,0,1:T(4,128)S(1)}, u32[]{:S(2)}, u32[]{:S(2)}) async-start(f32[3,16,256]{2,0,1:T(4,128)} %bitcast.58), calls=%async_computation.3 | async-start | bytes 131072 | tf_op jit(solution)/shard_map/all_to_all | solution.py:194
  120.5 10.8 %gather_fusion.9 = f32[4096,3]{1,0:T(8,128)S(1)} fusion(f32[3,1024]{0,1:T(8,128)S(1)} %copy.189, s32[4096]{0:T(1024)S(1)} %broadcast_clamp_fusion), kind=kCustom, calls=%fused_computation.9 | custom fusion | bytes 114688 | tf_op jit(solution)/shard_map/gather | solution.py:257
  131.4 1.2 copy.190
  132.7 1.4 fusion.101
  135.1 1.4 fusion.103
  137.4 6.7 %all-to-all-start.4 = ((f32[3,16,256]{2,0,1:T(4,128)}), f32[3,16,256]{2,0,1:T(4,128)S(1)}, u32[]{:S(2)}, u32[]{:S(2)}) async-start(f32[3,16,256]{2,0,1:T(4,128)} %bitcast.66), calls=%async_computation.4 | async-start | bytes 131072 | tf_op jit(solution)/shard_map/all_to_all | solution.py:195
  144.7 5.5 %gather_fusion.8 = f32[2048,3]{1,0:T(8,128)S(1)} fusion(f32[3,4096]{0,1:T(8,128)S(1)} %bitcast.292, s32[2048]{0:T(1024)S(1)} %broadcast_clamp_fusion.1), kind=kCustom, calls=%fused_computation.8 | custom fusion | bytes 57344 | tf_op jit(solution)/shard_map/gather | solution.py:217
  150.2 1.6 gather_fusion.7
  152.9 1.6 gather_fusion.10
  154.5 5.5 %gather_fusion.11 = f32[2048,3]{1,0:T(8,128)S(1)} fusion(f32[3,4096]{0,1:T(8,128)S(1)} %bitcast.289, s32[2048]{0:T(1024)S(1)} %broadcast_clamp_fusion.1), kind=kCustom, calls=%fused_computation.11 | custom fusion | bytes 57344 | tf_op jit(solution)/shard_map/gather | solution.py:218
  160.0 1.1 copy.186
  161.1 1.8 fusion.201
  162.8 1.1 copy.193
  166.2 8.7 %while.70 = (s32[]{:T(128)}, f32[9,32,128]{2,1,0:T(8,128)S(1)}, s32[5,512]{1,0:T(8,128)}, bf16[5,9,512]{2,1,0:T(8,128)(2,1)S(1)}, s32[]{:T(128)}, /*index=5*/s32[]{:T(128)}) while((s32[]{:T(128)}, f32[9,32,128]{2,1,0:T(8,128)S(1)}, s32[5,512]{1,0:T(8,128)}, bf16[5,9,512]{2,1,0:T(8,128)(2,1)S(1)}, s32[]{:T(128)}, ...), condition=%wide.region_35.36_spmd.clone, body=%wide.region_34.35_spmd.clone.sunk | while | flops 38503936 | bytes 468063 | solution.py:133
  175.7 6.0 %all-to-all-start.5 = ((f32[3,16,256]{2,0,1:T(4,128)}), f32[3,16,256]{2,0,1:T(4,128)S(1)}, u32[]{:S(2)}, u32[]{:S(2)}) async-start(f32[3,16,256]{2,0,1:T(4,128)} %bitcast.76), calls=%async_computation.5 | async-start | bytes 131072 | tf_op jit(solution)/shard_map/all_to_all | solution.py:202
  182.4 6.3 %all-to-all-done.5 = f32[3,16,256]{2,0,1:T(4,128)S(1)} async-done(((f32[3,16,256]{2,0,1:T(4,128)}), f32[3,16,256]{2,0,1:T(4,128)S(1)}, u32[]{:S(2)}, u32[]{:S(2)}) %all-to-all-start.5) | async-done | bytes 49184 | tf_op jit(solution)/shard_map/all_to_all | solution.py:202
  188.9 6.7 %while.71 = (s32[]{:T(128)}, f32[9,8,128]{2,1,0:T(8,128)S(1)}, s32[4,1024]{1,0:T(4,128)S(1)}, bf16[4,9,1024]{2,1,0:T(8,128)(2,1)S(1)}, s32[]{:T(128)}, /*index=5*/s32[]{:T(128)}) while((s32[]{:T(128)}, f32[9,8,128]{2,1,0:T(8,128)S(1)}, s32[4,1024]{1,0:T(4,128)S(1)}, bf16[4,9,1024]{2,1,0:T(8,128)(2,1)S(1)}, s32[]{:T(128)}, ...), condition=%wide.region_38.39_spmd.clone, body=%wide.region_37.38_spmd.clone.sunk | while | flops 20231172 | bytes 419935 | solution.py:133
  189.2 1.4 fusion.241
  190.9 1.4 fusion.241
  192.5 1.4 fusion.241
  194.2 1.4 fusion.241
  195.7 1.3 multiply_add_fusion
  (323 shorter events, 39.8 us)
Async XLA Ops:
  0.6 29.0 %copy-start.14 = (s32[1,16,256]{2,1,0:T(8,128)S(1)}, s32[1,16,256]{2,1,0:T(8,128)}, u32[]{:S(2)}) copy-start(s32[1,16,256]{2,1,0:T(8,128)} %param.31) | copy-start | bytes 49156
  0.6 21.2 %copy-start.1 = (f32[3,1024]{1,0:T(4,128)S(1)}, f32[3,1024]{1,0:T(4,128)}, u32[]{:S(2)}) copy-start(f32[3,1024]{1,0:T(4,128)} %param.24) | copy-start | bytes 36868
  0.7 26.6 %copy-start.28 = (s32[4,4,128]{2,1,0:T(4,128)S(1)}, s32[4,4,128]{2,1,0:T(4,128)}, u32[]{:S(2)}) copy-start(s32[4,4,128]{2,1,0:T(4,128)} %param.34) | copy-start | bytes 24580
  0.7 26.6 %copy-start.38 = (s32[4,128]{1,0:T(4,128)S(1)}, s32[4,128]{1,0:T(4,128)}, u32[]{:S(2)}) copy-start(s32[4,128]{1,0:T(4,128)} %param.33) | copy-start | bytes 6148
  0.7 27.8 %copy-start.37 = (f32[2,1024]{1,0:T(2,128)S(1)}, f32[2,1024]{1,0:T(2,128)}, u32[]{:S(2)}) copy-start(f32[2,1024]{1,0:T(2,128)} %param.28) | copy-start | bytes 24580
  0.7 28.1 %copy-start.39 = (f32[1024]{0:T(1024)S(1)}, f32[1024]{0:T(1024)}, u32[]{:S(2)}) copy-start(f32[1024]{0:T(1024)} %param.29) | copy-start | bytes 12292
  0.7 28.1 %copy-start.33 = (s32[4,1024]{1,0:T(4,128)S(1)}, s32[4,1024]{1,0:T(4,128)}, u32[]{:S(2)}) copy-start(s32[4,1024]{1,0:T(4,128)} %param.26) | copy-start | bytes 49156
  14.5 33.0 %all-to-all-start = ((f32[3,16,256]{2,0,1:T(4,128)}), f32[3,16,256]{2,0,1:T(4,128)S(1)}, u32[]{:S(2)}, u32[]{:S(2)}) async-start(f32[3,16,256]{2,0,1:T(4,128)} %bitcast.19), calls=%async_computation | async-start | bytes 131072 | tf_op jit(solution)/shard_map/all_to_all | solution.py:194
  21.9 20.7 %collective-permute-start = (f32[3,128]{1,0:T(4,128)S(1)}, f32[3,128]{1,0:T(4,128)S(1)}, u32[]{:S(2)}, u32[]{:S(2)}) collective-permute-start(f32[3,128]{1,0:T(4,128)S(1)} %slice.69), channel_id=1, source_target_pairs={{0,31},{1,0},{2,1},{3,2},{4,3},{5,4},{6,5},{7,6},{8,7},{9,8},{10,9... | collective-permute-start | bytes 4616 | tf_op jit(solution)/shard_map/ppermute | solution.py:21
  29.0 16.1 %copy-start.3 = (f32[3,1024]{1,0:T(4,128)}, f32[3,1024]{1,0:T(4,128)S(1)}, u32[]{:S(2)}) copy-start(f32[3,1024]{1,0:T(4,128)S(1)} %pad_maximum_fusion.10) | copy-start | bytes 36868
  29.1 16.0 %copy-start.7 = (f32[3,1024]{1,0:T(4,128)}, f32[3,1024]{1,0:T(4,128)S(1)}, u32[]{:S(2)}) copy-start(f32[3,1024]{1,0:T(4,128)S(1)} %maximum_maximum_fusion) | copy-start | bytes 36868
  41.3 3.0 %copy-start = (f32[8,1024]{1,0:T(8,128)S(1)}, f32[8,1024]{1,0:T(8,128)}, u32[]{:S(2)}) copy-start(f32[8,1024]{1,0:T(8,128)} %param.27) | copy-start | bytes 98308
  41.3 3.1 %copy-start.36 = (f32[3,1024]{1,0:T(4,128)S(1)}, f32[3,1024]{1,0:T(4,128)}, u32[]{:S(2)}) copy-start(f32[3,1024]{1,0:T(4,128)} %param.30) | copy-start | bytes 36868
  41.3 3.1 %copy-start.41 = (f32[4]{0:T(128)S(1)}, f32[4]{0:T(128)}, u32[]{:S(2)}) copy-start(f32[4]{0:T(128)} %constant.306.clone) | copy-start | bytes 52
  42.6 4.2 %copy-start.34 = (s32[4,8,128]{2,0,1:T(4,128)}, s32[4,8,128]{2,0,1:T(4,128)S(1)}, u32[]{:S(2)}) copy-start(s32[4,8,128]{2,0,1:T(4,128)S(1)} %copy.155) | copy-start | bytes 49156
  47.4 13.0 %all-to-all-start.1 = ((f32[3,16,256]{2,0,1:T(4,128)}), f32[3,16,256]{2,0,1:T(4,128)S(1)}, u32[]{:S(2)}, u32[]{:S(2)}) async-start(f32[3,16,256]{2,0,1:T(4,128)} %bitcast.29), calls=%async_computation.1 | async-start | bytes 131072 | tf_op jit(solution)/shard_map/all_to_all | solution.py:195
  57.1 3.9 %copy-start.17 = (s32[1024]{0:T(1024)S(1)}, s32[1024]{0:T(1024)}, u32[]{:S(2)}) copy-start(s32[1024]{0:T(1024)} %pad_clamp_fusion) | copy-start | bytes 12292
  61.1 11.3 %copy-start.27 = (f32[4,128,3]{1,2,0:T(4,128)S(1)}, f32[4,128,3]{1,2,0:T(4,128)}, u32[]{:S(2)}) copy-start(f32[4,128,3]{1,2,0:T(4,128)} %copy.172) | copy-start | bytes 18436
  72.1 2.3 %copy-start.10 = (f32[9,32,128]{2,1,0:T(8,128)S(1)}, f32[9,32,128]{2,1,0:T(8,128)}, u32[]{:S(2)}) copy-start(f32[9,32,128]{2,1,0:T(8,128)} %custom-call) | copy-start | bytes 442372
  74.4 15.5 %copy-start.15 = (f32[3,8,128]{2,1,0:T(8,128)S(1)}, f32[3,8,128]{2,1,0:T(8,128)}, u32[]{:S(2)}) copy-start(f32[3,8,128]{2,1,0:T(8,128)} %get-tuple-element.600) | copy-start | bytes 36868
  74.5 15.5 %copy-start.16 = (f32[3,8,128]{2,1,0:T(8,128)S(1)}, f32[3,8,128]{2,1,0:T(8,128)}, u32[]{:S(2)}) copy-start(f32[3,8,128]{2,1,0:T(8,128)} %get-tuple-element.601) | copy-start | bytes 36868
  74.5 22.6 %copy-start.26 = (f32[9,8,128]{2,1,0:T(8,128)S(1)}, f32[9,8,128]{2,1,0:T(8,128)}, u32[]{:S(2)}) copy-start(f32[9,8,128]{2,1,0:T(8,128)} %custom-call.1) | copy-start | bytes 110596
  84.0 12.9 %all-to-all-start.2 = ((f32[3,16,256]{2,0,1:T(4,128)}), f32[3,16,256]{2,0,1:T(4,128)S(1)}, u32[]{:S(2)}, u32[]{:S(2)}) async-start(f32[3,16,256]{2,0,1:T(4,128)} %bitcast.39), calls=%async_computation.2 | async-start | bytes 131072 | tf_op jit(solution)/shard_map/all_to_all | solution.py:202
  90.0 13.9 %collective-permute-start.1 = (f32[3,128]{1,0:T(4,128)S(1)}, f32[3,128]{1,0:T(4,128)S(1)}, u32[]{:S(2)}, u32[]{:S(2)}) collective-permute-start(f32[3,128]{1,0:T(4,128)S(1)} %slice.115), channel_id=1, source_target_pairs={{0,1},{1,2},{2,3},{3,4},{4,5},{5,6},{6,7},{7,8},{8,9},{9,10},{10,1... | collective-permute-start | bytes 4616 | tf_op jit(solution)/shard_map/ppermute | solution.py:21
  97.1 6.8 %copy-start.2 = (f32[3,1024]{1,0:T(4,128)S(1)}, f32[3,1024]{1,0:T(4,128)}, u32[]{:S(2)}) copy-start(f32[3,1024]{1,0:T(4,128)} %param.24) | copy-start | bytes 36868
  97.1 6.8 %copy-start.13 = (f32[3,1024]{1,0:T(4,128)S(1)}, f32[3,1024]{1,0:T(4,128)}, u32[]{:S(2)}) copy-start(f32[3,1024]{1,0:T(4,128)} %param.23) | copy-start | bytes 36868
  97.1 6.8 %copy-start.31 = (f32[1024]{0:T(1024)S(1)}, f32[1024]{0:T(1024)}, u32[]{:S(2)}) copy-start(f32[1024]{0:T(1024)} %param.25) | copy-start | bytes 12292
  103.9 27.4 %copy-start.5 = (f32[3,1024]{1,0:T(4,128)}, f32[3,1024]{1,0:T(4,128)S(1)}, u32[]{:S(2)}) copy-start(f32[3,1024]{1,0:T(4,128)S(1)} %get-tuple-element.584) | copy-start | bytes 36868
  104.0 28.7 %collective-permute-start.2 = (f32[3,128]{1,0:T(4,128)S(1)}, f32[3,128]{1,0:T(4,128)S(1)}, u32[]{:S(2)}, u32[]{:S(2)}) collective-permute-start(f32[3,128]{1,0:T(4,128)S(1)} %slice.116), channel_id=1, source_target_pairs={{0,31},{1,0},{2,1},{3,2},{4,3},{5,4},{6,5},{7,6},{8,7},{9,8},{10,9... | collective-permute-start | bytes 4616 | tf_op jit(solution)/shard_map/ppermute | solution.py:21
  115.6 17.1 %copy-start.35 = (s32[4,8,128]{2,0,1:T(4,128)S(1)}, s32[4,8,128]{2,0,1:T(4,128)}, u32[]{:S(2)}) copy-start(s32[4,8,128]{2,0,1:T(4,128)} %copy-done.34) | copy-start | bytes 49156
  116.8 20.5 %all-to-all-start.3 = ((f32[3,16,256]{2,0,1:T(4,128)}), f32[3,16,256]{2,0,1:T(4,128)S(1)}, u32[]{:S(2)}, u32[]{:S(2)}) async-start(f32[3,16,256]{2,0,1:T(4,128)} %bitcast.58), calls=%async_computation.3 | async-start | bytes 131072 | tf_op jit(solution)/shard_map/all_to_all | solution.py:194
  131.3 3.0 %copy-start.4 = (f32[3,1024]{1,0:T(4,128)S(1)}, f32[3,1024]{1,0:T(4,128)}, u32[]{:S(2)}) copy-start(f32[3,1024]{1,0:T(4,128)} %copy-done.3) | copy-start | bytes 36868
  131.3 3.0 %copy-start.8 = (f32[3,1024]{1,0:T(4,128)S(1)}, f32[3,1024]{1,0:T(4,128)}, u32[]{:S(2)}) copy-start(f32[3,1024]{1,0:T(4,128)} %copy-done.7) | copy-start | bytes 36868
  131.3 3.1 %copy-start.20 = (f32[1,1024]{1,0:T(1,128)S(1)}, f32[1,1024]{1,0:T(1,128)}, u32[]{:S(2)}) copy-start(f32[1,1024]{1,0:T(1,128)} %copy-done.19) | copy-start | bytes 12292
  131.3 3.1 %copy-start.22 = (f32[1,1024]{1,0:T(1,128)S(1)}, f32[1,1024]{1,0:T(1,128)}, u32[]{:S(2)}) copy-start(f32[1,1024]{1,0:T(1,128)} %copy-done.21) | copy-start | bytes 12292
  131.4 3.2 %copy-start.30 = (f32[4,1024]{1,0:T(4,128)S(1)}, f32[4,1024]{1,0:T(4,128)}, u32[]{:S(2)}) copy-start(f32[4,1024]{1,0:T(4,128)} %copy-done.29) | copy-start | bytes 49156
  131.4 3.2 %copy-start.42 = (f32[4]{0:T(128)S(1)}, f32[4]{0:T(128)}, u32[]{:S(2)}) copy-start(f32[4]{0:T(128)} %constant.306.clone) | copy-start | bytes 52
  135.1 15.0 %copy-start.18 = (s32[1024]{0:T(1024)S(1)}, s32[1024]{0:T(1024)}, u32[]{:S(2)}) copy-start(s32[1024]{0:T(1024)} %pad_clamp_fusion) | copy-start | bytes 12292
  136.7 15.5 %copy-start.11 = (f32[1,3,9,128]{3,1,2,0:T(4,128)}, f32[1,3,9,128]{3,1,2,0:T(4,128)S(1)}, u32[]{:S(2)}) copy-start(f32[1,3,9,128]{3,1,2,0:T(4,128)S(1)} %copy.229) | copy-start | bytes 41476
  137.3 58.4 %collective-permute-start.3 = (f32[3,128]{1,0:T(4,128)}, f32[3,128]{1,0:T(4,128)}, u32[]{:S(2)}, u32[]{:S(2)}) collective-permute-start(f32[3,128]{1,0:T(4,128)} %slice.122), channel_id=1, source_target_pairs={{0,1},{1,2},{2,3},{3,4},{4,5},{5,6},{6,7},{7,8},{8,9},{9,10},{10,1... | collective-permute-start | bytes 4616 | tf_op jit(solution)/shard_map/ppermute | solution.py:21
  137.4 14.8 %all-to-all-start.4 = ((f32[3,16,256]{2,0,1:T(4,128)}), f32[3,16,256]{2,0,1:T(4,128)S(1)}, u32[]{:S(2)}, u32[]{:S(2)}) async-start(f32[3,16,256]{2,0,1:T(4,128)} %bitcast.66), calls=%async_computation.4 | async-start | bytes 131072 | tf_op jit(solution)/shard_map/all_to_all | solution.py:195
  151.8 9.2 %copy-start.40 = (f32[4]{0:T(128)S(1)}, f32[4]{0:T(128)}, u32[]{:S(2)}) copy-start(f32[4]{0:T(128)} %compare_convert_fusion) | copy-start | bytes 52
  166.2 15.5 %copy-start.24 = (f32[1,1024]{1,0:T(1,128)S(1)}, f32[1,1024]{1,0:T(1,128)}, u32[]{:S(2)}) copy-start(f32[1,1024]{1,0:T(1,128)} %copy-done.23) | copy-start | bytes 12292
  166.2 22.7 %copy-start.25 = (f32[9,8,128]{2,1,0:T(8,128)S(1)}, f32[9,8,128]{2,1,0:T(8,128)}, u32[]{:S(2)}) copy-start(f32[9,8,128]{2,1,0:T(8,128)} %custom-call.3) | copy-start | bytes 110596
  175.7 12.9 %all-to-all-start.5 = ((f32[3,16,256]{2,0,1:T(4,128)}), f32[3,16,256]{2,0,1:T(4,128)S(1)}, u32[]{:S(2)}, u32[]{:S(2)}) async-start(f32[3,16,256]{2,0,1:T(4,128)} %bitcast.76), calls=%async_computation.5 | async-start | bytes 131072 | tf_op jit(solution)/shard_map/all_to_all | solution.py:202
  188.9 6.8 %copy-start.6 = (f32[3,1024]{1,0:T(4,128)S(1)}, f32[3,1024]{1,0:T(4,128)}, u32[]{:S(2)}) copy-start(f32[3,1024]{1,0:T(4,128)} %copy-done.5) | copy-start | bytes 36868
  188.9 6.8 %copy-start.12 = (f32[1,3,9,128]{3,1,2,0:T(4,128)S(1)}, f32[1,3,9,128]{3,1,2,0:T(4,128)}, u32[]{:S(2)}) copy-start(f32[1,3,9,128]{3,1,2,0:T(4,128)} %copy-done.11) | copy-start | bytes 41476
  188.9 6.8 %copy-start.32 = (f32[1024]{0:T(1024)S(1)}, f32[1024]{0:T(1024)}, u32[]{:S(2)}) copy-start(f32[1024]{0:T(1024)} %param.25) | copy-start | bytes 12292
  (5 other events, 4.7 us)
where the time goes:
time: 199 us; the launch traced here: 197 us
  local copies, waits for them, and re-layouts  97.6 us (49%)
  starting transfers between devices  39.5 us (20%)
  matrix products  32.1 us (16%)
  waiting for transfers between devices  12.7 us (6%)
  other arithmetic  11.6 us (6%)
  between operations  2.76 us (1%)
    gather x8, local copies, waits for them, and re-layouts, per_device(): recv_pos, recv_vel = ship_out(coords[:, slot_rows], velocity[:, slot_rows])  48 us
    dot_general x18, matrix products, add_block(): jnp.einsum('mh,kml->khl', high_match, spread_rows, preferred_element_type...  19.3 us
    all_to_all x2, waiting for transfers between devices, ship_back(): lax.all_to_all(buffer.reshape(3, group_size, capacity), ('wid', 'dep'), s...  12.6 us
    all_to_all x2, starting transfers between devices, ship_back(): lax.all_to_all(buffer.reshape(3, group_size, capacity), ('wid', 'dep'), s...  12 us
    all_to_all x2, starting transfers between devices, ship_out(): lax.all_to_all(positions, ('wid', 'dep'), split_axis=1, concat_axis=1, ti...  11.1 us
    gather x2, local copies, waits for them, and re-layouts, contact_buffer(): recv_pos[:, tile_facets]  10.9 us
    gather x2, local copies, waits for them, and re-layouts, contact_buffer(): recv_vel[:, tile_facets]  10.9 us
    all_to_all x2, starting transfers between devices, ship_out(): lax.all_to_all(velocities, ('wid', 'dep'), split_axis=1, concat_axis=1, t...  10.1 us
  transfers between devices with their start and end apart: 10, of which 2 were waited for; matrix products, arithmetic and copies ran while one was open for 52% of the time, Pallas kernels for 0%

commit v1 on v0

--- a/solution.py
+++ b/solution.py
@@ -191,7 +191,15 @@
 
 def ship_out(positions, velocities):
     recv_pos, recv_vel = (
-        lax.all_to_all(positions, ("wid", "dep"), split_axis=1, concat_axis=1, tiled=True),
+        jnp.concatenate(
+            lax.all_to_all(
+                jnp.stack(jnp.split(positions, lax.axis_size(("wid", "dep")), axis=1)),
+                ("wid", "dep"),
+                0,
+                0,
+            ),
+            axis=1,
+        ),
         lax.all_to_all(velocities, ("wid", "dep"), split_axis=1, concat_axis=1, tiled=True),
     )
     return (recv_pos.reshape(3, -1), recv_vel.reshape(3, -1))

time: 199 us -> 216 us (1.085)
  local copies, waits for them, and re-layouts: 97.6 us -> 115 us
    unnamed x95 -> x125, local copies, waits for them, and re-layouts: 2.33 us -> 20.1 us
  transfers between devices with their start and end apart: 10 -> 10, of which waited for: 2 -> 2; matrix products, arithmetic and copies ran while one was open for 52% -> 42% of each run, Pallas kernels for 0% -> 0%
where the time goes in v1:
time: 216 us; the launch traced here: 215 us
  local copies, waits for them, and re-layouts  115 us (53%)
  starting transfers between devices  39.4 us (18%)
  matrix products  32.1 us (15%)
  waiting for transfers between devices  12.7 us (6%)
  other arithmetic  11.6 us (5%)
  between operations  2.77 us (1%)
    gather x8, local copies, waits for them, and re-layouts, per_device(): recv_pos, recv_vel = ship_out(coords[:, slot_rows], velocity[:, slot_rows])  46.8 us
    unnamed x125, local copies, waits for them, and re-layouts  20.1 us
    dot_general x18, matrix products, add_block(): jnp.einsum('mh,kml->khl', high_match, spread_rows, preferred_element_type...  19.3 us
    all_to_all x2, waiting for transfers between devices, ship_back(): lax.all_to_all(buffer.reshape(3, group_size, capacity), ('wid', 'dep'), s...  12.6 us
    all_to_all x2, starting transfers between devices, ship_back(): lax.all_to_all(buffer.reshape(3, group_size, capacity), ('wid', 'dep'), s...  12 us
    all_to_all x2, starting transfers between devices, ship_out(): lax.all_to_all(jnp.stack(jnp.split(positions, lax.axis_size(('wid', 'dep'...  11.1 us
    gather x2, local copies, waits for them, and re-layouts, contact_buffer(): recv_pos[:, tile_facets]  10.9 us
    gather x2, local copies, waits for them, and re-layouts, contact_buffer(): recv_vel[:, tile_facets]  10.9 us
  transfers between devices with their start and end apart: 10, of which 2 were waited for; matrix products, arithmetic and copies ran while one was open for 42% of the time, Pallas kernels for 0%

profile of v1, /device:TPU:0, one launch (start us, length us, event | category | flops | bytes accessed | tf_op | source)
XLA Modules:
  0.0 214.6 jit_solution(2206209143662154894)
XLA Ops:
  0.7 1.0 copy.244
  2.4 10.8 %gather_fusion = f32[4096,3]{1,0:T(8,128)S(1)} fusion(f32[3,1024]{0,1:T(8,128)S(1)} %copy.244, s32[4096]{0:T(1024)S(1)} %broadcast_clamp_fusion), kind=kCustom, calls=%fused_computation | custom fusion | bytes 114688 | tf_op jit(solution)/shard_map/gather | solution.py:265
  23.3 7.4 %all-to-all-start = ((f32[16,3,1,256]{3,2,1,0:T(1,128)}), f32[16,3,1,256]{3,2,1,0:T(1,128)S(1)}, u32[]{:S(2)}, u32[]{:S(2)}) async-start(f32[16,3,1,256]{3,2,1,0:T(1,128)} %constant_dynamic-update-slice_fusion), calls=%async_computation | async-start | bytes 98304 | tf_op jit(solution)/shard_map/all_to_all | solution.py:195
  30.7 5.3 %collective-permute-start = (f32[3,128]{1,0:T(4,128)S(1)}, f32[3,128]{1,0:T(4,128)S(1)}, u32[]{:S(2)}, u32[]{:S(2)}) collective-permute-start(f32[3,128]{1,0:T(4,128)S(1)} %slice.69), channel_id=1, source_target_pairs={{0,31},{1,0},{2,1},{3,2},{4,3},{5,4},{6,5},{7,6},{8,7},{9,8},{10,9... | collective-permute-start | bytes 4616 | tf_op jit(solution)/shard_map/ppermute | solution.py:21
  39.4 10.8 %gather_fusion.3 = f32[4096,3]{1,0:T(8,128)S(1)} fusion(f32[3,1024]{0,1:T(8,128)S(1)} %copy.251, s32[4096]{0:T(1024)S(1)} %broadcast_clamp_fusion), kind=kCustom, calls=%fused_computation.3 | custom fusion | bytes 114688 | tf_op jit(solution)/shard_map/gather | solution.py:265
  50.2 1.2 copy.252
  51.5 1.4 fusion.100
  54.2 1.4 fusion.102
  56.2 3.5 %all-to-all-start.1 = ((f32[3,16,256]{2,0,1:T(4,128)}), f32[3,16,256]{2,0,1:T(4,128)S(1)}, u32[]{:S(2)}, u32[]{:S(2)}) async-start(f32[3,16,256]{2,0,1:T(4,128)} %bitcast.46), calls=%async_computation.1 | async-start | bytes 131072 | tf_op jit(solution)/shard_map/all_to_all | solution.py:203
  60.4 5.5 %gather_fusion.2 = f32[2048,3]{1,0:T(8,128)S(1)} fusion(f32[3,4096]{0,1:T(8,128)S(1)} %bitcast.416, s32[2048]{0:T(1024)S(1)} %broadcast_clamp_fusion.1), kind=kCustom, calls=%fused_computation.2 | custom fusion | bytes 57344 | tf_op jit(solution)/shard_map/gather | solution.py:225
  66.0 1.8 gather_fusion.1
  69.9 1.6 gather_fusion.4
  71.6 5.5 %gather_fusion.5 = f32[2048,3]{1,0:T(8,128)S(1)} fusion(f32[3,4096]{0,1:T(8,128)S(1)} %bitcast.421, s32[2048]{0:T(1024)S(1)} %broadcast_clamp_fusion.1), kind=kCustom, calls=%fused_computation.5 | custom fusion | bytes 57344 | tf_op jit(solution)/shard_map/gather | solution.py:226
  77.0 1.1 copy.248
  78.1 1.8 fusion.202
  79.9 1.1 copy.255
  83.3 8.7 %while.68 = (s32[]{:T(128)}, f32[9,32,128]{2,1,0:T(8,128)S(1)}, s32[5,512]{1,0:T(8,128)}, bf16[5,9,512]{2,1,0:T(8,128)(2,1)S(1)}, s32[]{:T(128)}, /*index=5*/s32[]{:T(128)}) while((s32[]{:T(128)}, f32[9,32,128]{2,1,0:T(8,128)S(1)}, s32[5,512]{1,0:T(8,128)}, bf16[5,9,512]{2,1,0:T(8,128)(2,1)S(1)}, s32[]{:T(128)}, ...), condition=%wide.region_15.16_spmd.clone, body=%wide.region_14.15_spmd.clone.sunk | while | flops 38503936 | bytes 468063 | solution.py:133
  84.2 0.8 fusion.232
  92.8 6.0 %all-to-all-start.2 = ((f32[3,16,256]{2,0,1:T(4,128)}), f32[3,16,256]{2,0,1:T(4,128)S(1)}, u32[]{:S(2)}, u32[]{:S(2)}) async-start(f32[3,16,256]{2,0,1:T(4,128)} %bitcast.56), calls=%async_computation.2 | async-start | bytes 131072 | tf_op jit(solution)/shard_map/all_to_all | solution.py:210
  99.3 6.4 %all-to-all-done.2 = f32[3,16,256]{2,0,1:T(4,128)S(1)} async-done(((f32[3,16,256]{2,0,1:T(4,128)}), f32[3,16,256]{2,0,1:T(4,128)S(1)}, u32[]{:S(2)}, u32[]{:S(2)}) %all-to-all-start.2) | async-done | bytes 49184 | tf_op jit(solution)/shard_map/all_to_all | solution.py:210
  106.0 6.7 %while.69 = (s32[]{:T(128)}, f32[9,8,128]{2,1,0:T(8,128)S(1)}, s32[4,1024]{1,0:T(4,128)S(1)}, bf16[4,9,1024]{2,1,0:T(8,128)(2,1)S(1)}, s32[]{:T(128)}, /*index=5*/s32[]{:T(128)}) while((s32[]{:T(128)}, f32[9,8,128]{2,1,0:T(8,128)S(1)}, s32[4,1024]{1,0:T(4,128)S(1)}, bf16[4,9,1024]{2,1,0:T(8,128)(2,1)S(1)}, s32[]{:T(128)}, ...), condition=%wide.region_18.19_spmd.clone, body=%wide.region_17.18_spmd.clone.sunk | while | flops 20231172 | bytes 419935 | solution.py:133
  106.3 1.4 fusion.235
  107.9 1.4 fusion.235
  109.6 1.4 fusion.235
  111.3 1.4 fusion.235
  113.0 10.8 %gather_fusion.6 = f32[4096,3]{1,0:T(8,128)S(1)} fusion(f32[3,1024]{0,1:T(8,128)S(1)} %copy.267, s32[4096]{0:T(1024)S(1)} %broadcast_clamp_fusion), kind=kCustom, calls=%fused_computation.6 | custom fusion | bytes 114688 | tf_op jit(solution)/shard_map/gather | solution.py:265
  134.5 3.7 %all-to-all-start.3 = ((f32[16,3,1,256]{3,2,1,0:T(1,128)}), f32[16,3,1,256]{3,2,1,0:T(1,128)S(1)}, u32[]{:S(2)}, u32[]{:S(2)}) async-start(f32[16,3,1,256]{3,2,1,0:T(1,128)} %constant_dynamic-update-slice_fusion.16), calls=%async_computation.3 | async-start | bytes 98304 | tf_op jit(solution)/shard_map/all_to_all | solution.py:195
  138.1 10.8 %gather_fusion.9 = f32[4096,3]{1,0:T(8,128)S(1)} fusion(f32[3,1024]{0,1:T(8,128)S(1)} %copy.274, s32[4096]{0:T(1024)S(1)} %broadcast_clamp_fusion), kind=kCustom, calls=%fused_computation.9 | custom fusion | bytes 114688 | tf_op jit(solution)/shard_map/gather | solution.py:265
  149.0 1.2 copy.275
  150.3 1.4 fusion.101
  152.8 1.4 fusion.103
  155.0 6.7 %all-to-all-start.4 = ((f32[3,16,256]{2,0,1:T(4,128)}), f32[3,16,256]{2,0,1:T(4,128)S(1)}, u32[]{:S(2)}, u32[]{:S(2)}) async-start(f32[3,16,256]{2,0,1:T(4,128)} %bitcast.100), calls=%async_computation.4 | async-start | bytes 131072 | tf_op jit(solution)/shard_map/all_to_all | solution.py:203
  162.3 5.5 %gather_fusion.8 = f32[2048,3]{1,0:T(8,128)S(1)} fusion(f32[3,4096]{0,1:T(8,128)S(1)} %bitcast.422, s32[2048]{0:T(1024)S(1)} %broadcast_clamp_fusion.1), kind=kCustom, calls=%fused_computation.8 | custom fusion | bytes 57344 | tf_op jit(solution)/shard_map/gather | solution.py:225
  167.8 1.6 gather_fusion.7
  170.5 1.6 gather_fusion.10
  172.1 5.5 %gather_fusion.11 = f32[2048,3]{1,0:T(8,128)S(1)} fusion(f32[3,4096]{0,1:T(8,128)S(1)} %bitcast.419, s32[2048]{0:T(1024)S(1)} %broadcast_clamp_fusion.1), kind=kCustom, calls=%fused_computation.11 | custom fusion | bytes 57344 | tf_op jit(solution)/shard_map/gather | solution.py:226
  177.6 1.1 copy.271
  178.7 1.7 fusion.201
  180.4 1.1 copy.278
  183.8 8.7 %while.70 = (s32[]{:T(128)}, f32[9,32,128]{2,1,0:T(8,128)S(1)}, s32[5,512]{1,0:T(8,128)}, bf16[5,9,512]{2,1,0:T(8,128)(2,1)S(1)}, s32[]{:T(128)}, /*index=5*/s32[]{:T(128)}) while((s32[]{:T(128)}, f32[9,32,128]{2,1,0:T(8,128)S(1)}, s32[5,512]{1,0:T(8,128)}, bf16[5,9,512]{2,1,0:T(8,128)(2,1)S(1)}, s32[]{:T(128)}, ...), condition=%wide.region_35.36_spmd.clone, body=%wide.region_34.35_spmd.clone.sunk | while | flops 38503936 | bytes 468063 | solution.py:133
  193.3 6.0 %all-to-all-start.5 = ((f32[3,16,256]{2,0,1:T(4,128)}), f32[3,16,256]{2,0,1:T(4,128)S(1)}, u32[]{:S(2)}, u32[]{:S(2)}) async-start(f32[3,16,256]{2,0,1:T(4,128)} %bitcast.110), calls=%async_computation.5 | async-start | bytes 131072 | tf_op jit(solution)/shard_map/all_to_all | solution.py:210
  200.0 6.3 %all-to-all-done.5 = f32[3,16,256]{2,0,1:T(4,128)S(1)} async-done(((f32[3,16,256]{2,0,1:T(4,128)}), f32[3,16,256]{2,0,1:T(4,128)S(1)}, u32[]{:S(2)}, u32[]{:S(2)}) %all-to-all-start.5) | async-done | bytes 49184 | tf_op jit(solution)/shard_map/all_to_all | solution.py:210
  206.5 6.7 %while.71 = (s32[]{:T(128)}, f32[9,8,128]{2,1,0:T(8,128)S(1)}, s32[4,1024]{1,0:T(4,128)S(1)}, bf16[4,9,1024]{2,1,0:T(8,128)(2,1)S(1)}, s32[]{:T(128)}, /*index=5*/s32[]{:T(128)}) while((s32[]{:T(128)}, f32[9,8,128]{2,1,0:T(8,128)S(1)}, s32[4,1024]{1,0:T(4,128)S(1)}, bf16[4,9,1024]{2,1,0:T(8,128)(2,1)S(1)}, s32[]{:T(128)}, ...), condition=%wide.region_38.39_spmd.clone, body=%wide.region_37.38_spmd.clone.sunk | while | flops 20231172 | bytes 419935 | solution.py:133
  206.8 1.4 fusion.241
  208.5 1.4 fusion.241
  210.1 1.4 fusion.241
  211.8 1.4 fusion.241
  213.3 1.3 multiply_add_fusion
  (355 shorter events, 58.1 us)
Async XLA Ops:
  0.6 37.8 %copy-start.14 = (s32[1,16,256]{2,1,0:T(8,128)S(1)}, s32[1,16,256]{2,1,0:T(8,128)}, u32[]{:S(2)}) copy-start(s32[1,16,256]{2,1,0:T(8,128)} %param.31) | copy-start | bytes 49156
  0.6 30.1 %copy-start.1 = (f32[3,1024]{1,0:T(4,128)S(1)}, f32[3,1024]{1,0:T(4,128)}, u32[]{:S(2)}) copy-start(f32[3,1024]{1,0:T(4,128)} %param.24) | copy-start | bytes 36868
  0.7 35.4 %copy-start.28 = (s32[4,4,128]{2,1,0:T(4,128)S(1)}, s32[4,4,128]{2,1,0:T(4,128)}, u32[]{:S(2)}) copy-start(s32[4,4,128]{2,1,0:T(4,128)} %param.34) | copy-start | bytes 24580
  0.7 35.4 %copy-start.38 = (s32[4,128]{1,0:T(4,128)S(1)}, s32[4,128]{1,0:T(4,128)}, u32[]{:S(2)}) copy-start(s32[4,128]{1,0:T(4,128)} %param.33) | copy-start | bytes 6148
  0.7 36.7 %copy-start.37 = (f32[2,1024]{1,0:T(2,128)S(1)}, f32[2,1024]{1,0:T(2,128)}, u32[]{:S(2)}) copy-start(f32[2,1024]{1,0:T(2,128)} %param.28) | copy-start | bytes 24580
  0.7 36.9 %copy-start.39 = (f32[1024]{0:T(1024)S(1)}, f32[1024]{0:T(1024)}, u32[]{:S(2)}) copy-start(f32[1024]{0:T(1024)} %param.29) | copy-start | bytes 12292
  0.7 37.0 %copy-start.33 = (s32[4,1024]{1,0:T(4,128)S(1)}, s32[4,1024]{1,0:T(4,128)}, u32[]{:S(2)}) copy-start(s32[4,1024]{1,0:T(4,128)} %param.26) | copy-start | bytes 49156
  23.3 32.9 %all-to-all-start = ((f32[16,3,1,256]{3,2,1,0:T(1,128)}), f32[16,3,1,256]{3,2,1,0:T(1,128)S(1)}, u32[]{:S(2)}, u32[]{:S(2)}) async-start(f32[16,3,1,256]{3,2,1,0:T(1,128)} %constant_dynamic-update-slice_fusion), calls=%async_computation | async-start | bytes 98304 | tf_op jit(solution)/shard_map/all_to_all | solution.py:195
  30.7 20.7 %collective-permute-start = (f32[3,128]{1,0:T(4,128)S(1)}, f32[3,128]{1,0:T(4,128)S(1)}, u32[]{:S(2)}, u32[]{:S(2)}) collective-permute-start(f32[3,128]{1,0:T(4,128)S(1)} %slice.69), channel_id=1, source_target_pairs={{0,31},{1,0},{2,1},{3,2},{4,3},{5,4},{6,5},{7,6},{8,7},{9,8},{10,9... | collective-permute-start | bytes 4616 | tf_op jit(solution)/shard_map/ppermute | solution.py:21
  37.8 16.0 %copy-start.3 = (f32[3,1024]{1,0:T(4,128)}, f32[3,1024]{1,0:T(4,128)S(1)}, u32[]{:S(2)}) copy-start(f32[3,1024]{1,0:T(4,128)S(1)} %pad_maximum_fusion.10) | copy-start | bytes 36868
  37.9 16.0 %copy-start.7 = (f32[3,1024]{1,0:T(4,128)}, f32[3,1024]{1,0:T(4,128)S(1)}, u32[]{:S(2)}) copy-start(f32[3,1024]{1,0:T(4,128)S(1)} %maximum_maximum_fusion) | copy-start | bytes 36868
  50.1 3.0 %copy-start = (f32[8,1024]{1,0:T(8,128)S(1)}, f32[8,1024]{1,0:T(8,128)}, u32[]{:S(2)}) copy-start(f32[8,1024]{1,0:T(8,128)} %param.27) | copy-start | bytes 98308
  50.1 3.1 %copy-start.36 = (f32[3,1024]{1,0:T(4,128)S(1)}, f32[3,1024]{1,0:T(4,128)}, u32[]{:S(2)}) copy-start(f32[3,1024]{1,0:T(4,128)} %param.30) | copy-start | bytes 36868
  50.2 3.1 %copy-start.41 = (f32[4]{0:T(128)S(1)}, f32[4]{0:T(128)}, u32[]{:S(2)}) copy-start(f32[4]{0:T(128)} %constant.306.clone) | copy-start | bytes 52
  51.4 4.2 %copy-start.34 = (s32[4,8,128]{2,0,1:T(4,128)}, s32[4,8,128]{2,0,1:T(4,128)S(1)}, u32[]{:S(2)}) copy-start(s32[4,8,128]{2,0,1:T(4,128)S(1)} %copy.240) | copy-start | bytes 49156
  56.2 13.0 %all-to-all-start.1 = ((f32[3,16,256]{2,0,1:T(4,128)}), f32[3,16,256]{2,0,1:T(4,128)S(1)}, u32[]{:S(2)}, u32[]{:S(2)}) async-start(f32[3,16,256]{2,0,1:T(4,128)} %bitcast.46), calls=%async_computation.1 | async-start | bytes 131072 | tf_op jit(solution)/shard_map/all_to_all | solution.py:203
  66.0 4.0 %copy-start.17 = (s32[1024]{0:T(1024)S(1)}, s32[1024]{0:T(1024)}, u32[]{:S(2)}) copy-start(s32[1024]{0:T(1024)} %pad_clamp_fusion) | copy-start | bytes 12292
  69.9 11.3 %copy-start.27 = (f32[4,128,3]{1,2,0:T(4,128)S(1)}, f32[4,128,3]{1,2,0:T(4,128)}, u32[]{:S(2)}) copy-start(f32[4,128,3]{1,2,0:T(4,128)} %copy.257) | copy-start | bytes 18436
  80.9 2.3 %copy-start.10 = (f32[9,32,128]{2,1,0:T(8,128)S(1)}, f32[9,32,128]{2,1,0:T(8,128)}, u32[]{:S(2)}) copy-start(f32[9,32,128]{2,1,0:T(8,128)} %custom-call) | copy-start | bytes 442372
  83.3 15.5 %copy-start.15 = (f32[3,8,128]{2,1,0:T(8,128)S(1)}, f32[3,8,128]{2,1,0:T(8,128)}, u32[]{:S(2)}) copy-start(f32[3,8,128]{2,1,0:T(8,128)} %get-tuple-element.619) | copy-start | bytes 36868
  83.3 15.5 %copy-start.16 = (f32[3,8,128]{2,1,0:T(8,128)S(1)}, f32[3,8,128]{2,1,0:T(8,128)}, u32[]{:S(2)}) copy-start(f32[3,8,128]{2,1,0:T(8,128)} %get-tuple-element.620) | copy-start | bytes 36868
  83.3 22.6 %copy-start.26 = (f32[9,8,128]{2,1,0:T(8,128)S(1)}, f32[9,8,128]{2,1,0:T(8,128)}, u32[]{:S(2)}) copy-start(f32[9,8,128]{2,1,0:T(8,128)} %custom-call.1) | copy-start | bytes 110596
  92.8 12.9 %all-to-all-start.2 = ((f32[3,16,256]{2,0,1:T(4,128)}), f32[3,16,256]{2,0,1:T(4,128)S(1)}, u32[]{:S(2)}, u32[]{:S(2)}) async-start(f32[3,16,256]{2,0,1:T(4,128)} %bitcast.56), calls=%async_computation.2 | async-start | bytes 131072 | tf_op jit(solution)/shard_map/all_to_all | solution.py:210
  98.8 13.9 %collective-permute-start.1 = (f32[3,128]{1,0:T(4,128)S(1)}, f32[3,128]{1,0:T(4,128)S(1)}, u32[]{:S(2)}, u32[]{:S(2)}) collective-permute-start(f32[3,128]{1,0:T(4,128)S(1)} %slice.115), channel_id=1, source_target_pairs={{0,1},{1,2},{2,3},{3,4},{4,5},{5,6},{6,7},{7,8},{8,9},{9,10},{10,1... | collective-permute-start | bytes 4616 | tf_op jit(solution)/shard_map/ppermute | solution.py:21
  105.9 6.8 %copy-start.2 = (f32[3,1024]{1,0:T(4,128)S(1)}, f32[3,1024]{1,0:T(4,128)}, u32[]{:S(2)}) copy-start(f32[3,1024]{1,0:T(4,128)} %param.24) | copy-start | bytes 36868
  106.0 6.8 %copy-start.13 = (f32[3,1024]{1,0:T(4,128)S(1)}, f32[3,1024]{1,0:T(4,128)}, u32[]{:S(2)}) copy-start(f32[3,1024]{1,0:T(4,128)} %param.23) | copy-start | bytes 36868
  106.0 6.8 %copy-start.31 = (f32[1024]{0:T(1024)S(1)}, f32[1024]{0:T(1024)}, u32[]{:S(2)}) copy-start(f32[1024]{0:T(1024)} %param.25) | copy-start | bytes 12292
  112.8 11.0 %copy-start.5 = (f32[3,1024]{1,0:T(4,128)}, f32[3,1024]{1,0:T(4,128)S(1)}, u32[]{:S(2)}) copy-start(f32[3,1024]{1,0:T(4,128)S(1)} %get-tuple-element.603) | copy-start | bytes 36868
  124.4 25.9 %copy-start.35 = (s32[4,8,128]{2,0,1:T(4,128)S(1)}, s32[4,8,128]{2,0,1:T(4,128)}, u32[]{:S(2)}) copy-start(s32[4,8,128]{2,0,1:T(4,128)} %copy-done.34) | copy-start | bytes 49156
  133.3 16.9 %collective-permute-start.2 = (f32[3,128]{1,0:T(4,128)S(1)}, f32[3,128]{1,0:T(4,128)S(1)}, u32[]{:S(2)}, u32[]{:S(2)}) collective-permute-start(f32[3,128]{1,0:T(4,128)S(1)} %slice.116), channel_id=1, source_target_pairs={{0,31},{1,0},{2,1},{3,2},{4,3},{5,4},{6,5},{7,6},{8,7},{9,8},{10,9... | collective-permute-start | bytes 4616 | tf_op jit(solution)/shard_map/ppermute | solution.py:21
  134.5 20.5 %all-to-all-start.3 = ((f32[16,3,1,256]{3,2,1,0:T(1,128)}), f32[16,3,1,256]{3,2,1,0:T(1,128)S(1)}, u32[]{:S(2)}, u32[]{:S(2)}) async-start(f32[16,3,1,256]{3,2,1,0:T(1,128)} %constant_dynamic-update-slice_fusion.16), calls=%async_computation.3 | async-start | bytes 98304 | tf_op jit(solution)/shard_map/all_to_all | solution.py:195
  148.9 3.0 %copy-start.4 = (f32[3,1024]{1,0:T(4,128)S(1)}, f32[3,1024]{1,0:T(4,128)}, u32[]{:S(2)}) copy-start(f32[3,1024]{1,0:T(4,128)} %copy-done.3) | copy-start | bytes 36868
  148.9 3.0 %copy-start.8 = (f32[3,1024]{1,0:T(4,128)S(1)}, f32[3,1024]{1,0:T(4,128)}, u32[]{:S(2)}) copy-start(f32[3,1024]{1,0:T(4,128)} %copy-done.7) | copy-start | bytes 36868
  148.9 3.1 %copy-start.20 = (f32[1,1024]{1,0:T(1,128)S(1)}, f32[1,1024]{1,0:T(1,128)}, u32[]{:S(2)}) copy-start(f32[1,1024]{1,0:T(1,128)} %copy-done.19) | copy-start | bytes 12292
  149.0 3.1 %copy-start.22 = (f32[1,1024]{1,0:T(1,128)S(1)}, f32[1,1024]{1,0:T(1,128)}, u32[]{:S(2)}) copy-start(f32[1,1024]{1,0:T(1,128)} %copy-done.21) | copy-start | bytes 12292
  149.0 3.2 %copy-start.30 = (f32[4,1024]{1,0:T(4,128)S(1)}, f32[4,1024]{1,0:T(4,128)}, u32[]{:S(2)}) copy-start(f32[4,1024]{1,0:T(4,128)} %copy-done.29) | copy-start | bytes 49156
  149.0 3.2 %copy-start.42 = (f32[4]{0:T(128)S(1)}, f32[4]{0:T(128)}, u32[]{:S(2)}) copy-start(f32[4]{0:T(128)} %constant.306.clone) | copy-start | bytes 52
  152.7 15.0 %copy-start.18 = (s32[1024]{0:T(1024)S(1)}, s32[1024]{0:T(1024)}, u32[]{:S(2)}) copy-start(s32[1024]{0:T(1024)} %pad_clamp_fusion) | copy-start | bytes 12292
  154.3 15.5 %copy-start.11 = (f32[1,3,9,128]{3,1,2,0:T(4,128)}, f32[1,3,9,128]{3,1,2,0:T(4,128)S(1)}, u32[]{:S(2)}) copy-start(f32[1,3,9,128]{3,1,2,0:T(4,128)S(1)} %copy.314) | copy-start | bytes 41476
  154.9 58.4 %collective-permute-start.3 = (f32[3,128]{1,0:T(4,128)}, f32[3,128]{1,0:T(4,128)}, u32[]{:S(2)}, u32[]{:S(2)}) collective-permute-start(f32[3,128]{1,0:T(4,128)} %slice.122), channel_id=1, source_target_pairs={{0,1},{1,2},{2,3},{3,4},{4,5},{5,6},{6,7},{7,8},{8,9},{9,10},{10,1... | collective-permute-start | bytes 4616 | tf_op jit(solution)/shard_map/ppermute | solution.py:21
  155.0 14.8 %all-to-all-start.4 = ((f32[3,16,256]{2,0,1:T(4,128)}), f32[3,16,256]{2,0,1:T(4,128)S(1)}, u32[]{:S(2)}, u32[]{:S(2)}) async-start(f32[3,16,256]{2,0,1:T(4,128)} %bitcast.100), calls=%async_computation.4 | async-start | bytes 131072 | tf_op jit(solution)/shard_map/all_to_all | solution.py:203
  169.4 9.2 %copy-start.40 = (f32[4]{0:T(128)S(1)}, f32[4]{0:T(128)}, u32[]{:S(2)}) copy-start(f32[4]{0:T(128)} %compare_convert_fusion) | copy-start | bytes 52
  183.8 15.5 %copy-start.24 = (f32[1,1024]{1,0:T(1,128)S(1)}, f32[1,1024]{1,0:T(1,128)}, u32[]{:S(2)}) copy-start(f32[1,1024]{1,0:T(1,128)} %copy-done.23) | copy-start | bytes 12292
  183.8 22.7 %copy-start.25 = (f32[9,8,128]{2,1,0:T(8,128)S(1)}, f32[9,8,128]{2,1,0:T(8,128)}, u32[]{:S(2)}) copy-start(f32[9,8,128]{2,1,0:T(8,128)} %custom-call.3) | copy-start | bytes 110596
  193.3 12.9 %all-to-all-start.5 = ((f32[3,16,256]{2,0,1:T(4,128)}), f32[3,16,256]{2,0,1:T(4,128)S(1)}, u32[]{:S(2)}, u32[]{:S(2)}) async-start(f32[3,16,256]{2,0,1:T(4,128)} %bitcast.110), calls=%async_computation.5 | async-start | bytes 131072 | tf_op jit(solution)/shard_map/all_to_all | solution.py:210
  206.5 6.8 %copy-start.6 = (f32[3,1024]{1,0:T(4,128)S(1)}, f32[3,1024]{1,0:T(4,128)}, u32[]{:S(2)}) copy-start(f32[3,1024]{1,0:T(4,128)} %copy-done.5) | copy-start | bytes 36868
  206.5 6.8 %copy-start.12 = (f32[1,3,9,128]{3,1,2,0:T(4,128)S(1)}, f32[1,3,9,128]{3,1,2,0:T(4,128)}, u32[]{:S(2)}) copy-start(f32[1,3,9,128]{3,1,2,0:T(4,128)} %copy-done.11) | copy-start | bytes 41476
  206.5 6.8 %copy-start.32 = (f32[1024]{0:T(1024)S(1)}, f32[1024]{0:T(1024)}, u32[]{:S(2)}) copy-start(f32[1024]{0:T(1024)} %param.25) | copy-start | bytes 12292
  (5 other events, 4.7 us)
